TPU v7x, 256 devices: a whole 4x4x8 slice. The times are simulated.
256 devices in a mesh: dp: 4 (over x), expert: 64 (over z, y, core).
Axes of the slice: x: 4, y: 4, z: 8, core: 2. Of those that a mesh axis runs over, the one named last changes fastest.
Arguments:
- tokens: bfloat16 [32768, 2048], P(('dp', 'expert')), may hold values from -6 to 6
- expert_ids: int32 [32768, 2], P(('dp', 'expert')), may hold values from 0 to 63, all different within a row; in each aligned block of 128 rows (0 to 127, 128 to 255, ...) at most 5 rows name the same one
- gate_units: int32 [32768, 2], P(('dp', 'expert')), may hold values from 64 to 1023
- capacity: int32 [64], replicated, may hold values from 512 to 1535
- w_gate: bfloat16 [64, 2048, 1408], P('expert', None, 'dp'), may hold values from -0.125 to 0.125
- w_up: bfloat16 [64, 2048, 1408], P('expert', None, 'dp'), may hold values from -0.125 to 0.125
- w_down: bfloat16 [64, 2048, 1408], P('expert', None, 'dp'), may hold values from -0.15625 to 0.15625
Outputs:
- mixed: bfloat16 [32768, 2048], P(('dp', 'expert'))
Inputs may be any that keep to these rules, and one draw needn't show every extreme that they name: `expert_ids`: each row names two different experts; of one device's 128 rows (aligned blocks) no expert is named more than 5 times.
All inputs are finite; a program needn't handle non-finite values.
Results may differ from a plain program's by a relative error of at most 0.0057.
Values may be sent and summed in bfloat16 or wider, within the bound.
A program may use at most 128 MiB of HBM per device.

v0:
```python
import jax
import jax.numpy as jnp
from jax import lax
from jax.sharding import Mesh
from jax.sharding import PartitionSpec as P

DP_EXPERT = ("dp", "expert_0", "expert_1", "expert_2")
EXPERT = ("expert_0", "expert_1", "expert_2")


def neutral_like(shard, identity):
    return jnp.zeros_like(shard) + jnp.asarray(identity, shard.dtype)


def carried_in(shard, axes, combine, identity):
    before = start = neutral_like(shard, identity)
    total = shard
    for axis in reversed(axes):
        length, here = (lax.axis_size(axis), lax.axis_index(axis))
        pieces = lax.all_gather(total, axis)
        inside, total = (start, start)
        for k in range(length):
            passed = k < here
            total = combine(total, pieces[k])
            inside = jnp.where(passed, total, inside)
        before = combine(inside, before)
    return before


def gather_turned(arrays, axis, dims):
    turned = [jnp.moveaxis(a, dim, 0) for a, dim in zip(arrays, dims)]
    both = jnp.concatenate([t.reshape(len(t), -1) for t in turned], axis=1)
    filled, at, finished = (lax.all_gather(both, axis, axis=0, tiled=True), 0, [])
    for t, dim in zip(turned, dims):
        piece = filled[:, at : at + t[0].size].reshape(-1, *t.shape[1:])
        finished.append(jnp.moveaxis(piece, 0, dim))
        at += t[0].size
    return tuple(finished)


def expert_rows(rows, gate_w, up_w, down_w):
    gate = jnp.dot(rows, gate_w, preferred_element_type=jnp.float32)
    up = jnp.dot(rows, up_w, preferred_element_type=jnp.float32)
    hidden = (jax.nn.silu(gate) * up).astype(jnp.bfloat16)
    return lax.dot_general(
        hidden, down_w, (((1,), (1,)), ((), ())), preferred_element_type=jnp.float32
    )


def add_counts(earlier, later):
    return earlier + later


def local(tokens, expert_ids, gate_units, capacity, w_gate, w_up, w_down):
    tok_rows = tokens.shape[0]
    width = tokens.shape[1]
    n_experts = capacity.shape[0]
    most = max(2, 5 * tok_rows // (2 * n_experts))
    slots_all = n_experts * most
    flat = expert_ids.reshape(-1)
    onehot = (flat[:, None] == jnp.arange(n_experts, dtype=jnp.int32)[None, :]).astype(jnp.int32)
    local_rank = jnp.sum((jnp.cumsum(onehot, axis=0) - onehot) * onehot, axis=1)
    counts = jnp.sum(onehot, axis=0)
    offsets = carried_in(counts, DP_EXPERT, add_counts, jnp.zeros_like(counts))
    global_slot = jnp.sum(onehot * offsets[None, :], axis=1) + local_rank
    limit = jnp.sum(onehot * capacity[None, :], axis=1)
    kept = global_slot < limit
    weight = jnp.where(kept, gate_units.reshape(-1).astype(jnp.float32) / 1024.0, jnp.float32(0.0))
    send_slot = flat * most + local_rank
    chosen = (send_slot[None, :] == jnp.arange(slots_all, dtype=jnp.int32)[:, None]) & kept[None, :]
    placing = jnp.sum(chosen.reshape(slots_all, tok_rows, 2).astype(jnp.int32), axis=2).astype(
        jnp.bfloat16
    )
    outgoing = jnp.dot(placing, tokens, preferred_element_type=jnp.float32).astype(jnp.bfloat16)
    outgoing = outgoing.reshape(n_experts, most, width)
    arrived = lax.all_to_all(outgoing, EXPERT, split_axis=0, concat_axis=0, tiled=True).reshape(
        slots_all, width
    )
    pieces = gather_turned((w_gate, w_up, w_down), "dp", (2, 2, 2))
    produced = expert_rows(arrived, pieces[0][0], pieces[1][0], pieces[2][0])
    answer = produced.astype(jnp.bfloat16).reshape(n_experts, most, width)
    back = lax.all_to_all(answer, EXPERT, split_axis=0, concat_axis=0, tiled=True).reshape(
        slots_all, width
    )
    picked = back[send_slot].astype(jnp.float32) * weight[:, None]
    mixed = jnp.sum(picked.reshape(tok_rows, 2, width), axis=1)
    return mixed.astype(jnp.bfloat16)


def solution(mesh):
    finer = Mesh(
        mesh.devices.reshape(mesh.shape["dp"], 8, 4, 2), ("dp", "expert_0", "expert_1", "expert_2")
    )
    return jax.shard_map(
        local,
        mesh=finer,
        in_specs=(
            P(DP_EXPERT, None),
            P(DP_EXPERT, None),
            P(DP_EXPERT, None),
            P(),
            P(EXPERT, None, "dp"),
            P(EXPERT, None, "dp"),
            P(EXPERT, None, "dp"),
        ),
        out_specs=P(DP_EXPERT, None),
        check_vma=False,
    )
```

profile of v0, /device:TPU:8, one launch (start us, length us, event | category | flops | bytes accessed | tf_op | source)
XLA Modules:
  0.0 272.6 jit_solution(670092717847320149)
XLA Ops:
  6.5 3.8 %pad_maximum_fusion = bf16[352,6144]{1,0:T(8,128)(2,1)} fusion(bf16[352,2048]{1,0:T(8,128)(2,1)} %bitcast.106, bf16[352,2048]{1,0:T(8,128)(2,1)} %bitcast.107, bf16[352,2048]{1,0:T(8,128)(2,1)} %bitcast.108), kind=kLoop, calls=%fused_computation.7 | loop fusion | flops 12976128 | bytes 8650752 | tf_op jit(solution)/shard_map/concatenate | solution.py:32
  10.5 0.6 copy-done.1
  11.2 0.1 eq.39
  11.3 0.1 eq.43
  11.5 0.6 dynamic-slice.1
  12.1 0.7 dynamic-slice
  14.1 0.6 reduce-window.6
  14.7 0.2 slice_reduce_fusion
  15.1 0.2 dynamic-update-slice
  15.3 1.8 all-reduce
  17.1 0.2 fusion.26
  17.3 8.2 %all-reduce.1 = s32[256]{0:T(256)S(1)} all-reduce(s32[256]{0:T(256)S(1)} %fusion.26), channel_id=3, replica_groups=mesh['dp'=4,'expert_0'=8,'expert_1'=4,'expert_2'=2] {'expert_1'}, use_global_device_ids=true, to_apply=%add.1 | all-reduce | flops 256 | bytes 2048
  25.5 19.1 %all-gather.2 = s32[8,1,64]{2,1,0:T(1,128)S(1)} all-gather(s32[1,1,64]{2,1,0:T(1,128)S(1)} %fusion.32), channel_id=1, replica_groups=mesh['dp'=4,'expert_0'=8,'expert_1'=4,'expert_2'=2] {'expert_0'}, dimensions={0}, use_global_device_ids=true | all-gather | bytes 2304 | tf_op jit(solution)/shard_map/all_gather | solution.py:20
  44.7 10.0 %all-gather.3 = s32[4,1,64]{2,1,0:T(1,128)S(1)} all-gather(s32[1,1,64]{2,1,0:T(1,128)S(1)} %bitcast.110), channel_id=1, replica_groups=mesh['dp'=4,'expert_0'=8,'expert_1'=4,'expert_2'=2] {'dp'}, dimensions={0}, use_global_device_ids=true | all-gather | bytes 1280 | tf_op jit(solution)/shard_map/all_gather | solution.py:20
  54.8 0.1 reduce_sum.63
  55.1 0.2 reduce_sum.68
  55.4 0.2 reduce_sum.66
  55.7 1.6 convolution_convert_fusion
  57.3 2.4 reshape.138
  59.7 57.2 %all_to_all.10 = bf16[64,5,2048]{2,1,0:T(8,128)(2,1)} all-to-all(bf16[64,5,2048]{2,1,0:T(8,128)(2,1)S(1)} %reshape.138), channel_id=1, replica_groups=mesh['dp'=4,'expert_0'=8,'expert_1'=4,'expert_2'=2] {'expert_0','expert_..., dimensions={0} | all-to-all | bytes 2621440 | tf_op jit(solution)/shard_map/all_to_all | solution.py:76
  116.8 2.6 reshape.139
  119.4 56.2 %all-gather.6.cloned.1.call-done = bf16[1408,6144]{1,0:T(8,128)(2,1)} async-done(((bf16[352,6144]{1,0:T(8,128)(2,1)}), bf16[1408,6144]{1,0:T(8,128)(2,1)}) %all-gather.6.cloned.1.call-update) | async-done | bytes 17301520 | tf_op jit(solution)/shard_map/all_gather | solution.py:33
  175.6 6.1 %fusion.2 = f32[320,1408]{1,0:T(8,128)} fusion(bf16[320,2048]{1,0:T(8,128)(2,1)S(1)} %reshape.139, bf16[1408,6144]{1,0:T(8,128)(2,1)} %all-gather.6.cloned.1.call-done), kind=kOutput, calls=%fused_computation.6 | convolution fusion | flops 1845493760 | bytes 8880128 | tf_op jit(solution)/shard_map/dot_general | solution.py:42
  181.7 9.2 %fusion.4 = bf16[320,2048]{1,0:T(8,128)(2,1)S(1)} fusion(bf16[1408,6144]{1,0:T(8,128)(2,1)} %all-gather.6.cloned.1.call-done, bf16[320,2048]{1,0:T(8,128)(2,1)S(1)} %reshape.139, f32[320,1408]{1,0:T(8,128)} %fusion.2), kind=kOutput, calls=%fused_computation.9 | convolution fusion | flops 3694346240 | bytes 15958016 | tf_op jit(solution)/shard_map/dot_general | solution.py:45
  190.9 1.6 reshape.146
  192.5 10.8 %all-to-all-start.1 = ((bf16[64,5,2048]{2,1,0:T(8,128)(2,1)}), bf16[64,5,2048]{2,1,0:T(8,128)(2,1)}, u32[]{:S(2)}, u32[]{:S(2)}) async-start(bf16[64,5,2048]{2,1,0:T(8,128)(2,1)} %reshape.146), calls=%async_computation.1 | async-start | bytes 4194304 | tf_op jit(solution)/shard_map/all_to_all | solution.py:82
  203.2 0.1 mul.67
  203.5 50.9 %all-to-all-done.1 = bf16[64,5,2048]{2,1,0:T(8,128)(2,1)} async-done(((bf16[64,5,2048]{2,1,0:T(8,128)(2,1)}), bf16[64,5,2048]{2,1,0:T(8,128)(2,1)}, u32[]{:S(2)}, u32[]{:S(2)}) %all-to-all-start.1) | async-done | bytes 1310752 | tf_op jit(solution)/shard_map/all_to_all | solution.py:82
  254.4 2.6 reshape.147
  256.9 2.3 gather_fusion
  259.3 2.4 reshape.148
  261.7 4.0 %multiply_reduce_fusion = bf16[128,2048]{1,0:T(8,128)(2,1)} fusion(f32[128,2,2048]{2,1,0:T(2,128)S(1)} %reshape.148, f32[128,2]{1,0:T(8,128)S(1)} %copy.39), kind=kLoop, calls=%fused_computation.12 | loop fusion | flops 786432 | bytes 2622464 | tf_op jit(solution)/shard_map/reduce_sum | solution.py:86
  (34 shorter events, 1.1 us)
Async XLA Ops:
  6.5 49.1 %copy-start = (bf16[128,2048]{1,0:T(8,128)(2,1)S(1)}, bf16[128,2048]{1,0:T(8,128)(2,1)}, u32[]{:S(2)}) copy-start(bf16[128,2048]{1,0:T(8,128)(2,1)} %param.7) | copy-start | bytes 1572868
  6.5 169.1 %all-gather.6.cloned.1.call-start = ((), (), s32[]{:S(2)}) async-start(), calls=%async_computation.2 | async-start | bytes 21626880 | tf_op jit(solution)/shard_map/all_gather | solution.py:33
  10.4 0.7 copy-start.1
  10.4 1.1 copy-start.5
  10.4 1.7 copy-start.4
  10.4 44.3 %copy-start.3 = (s32[64]{0:T(128)S(1)}, s32[64]{0:T(128)}, u32[]{:S(2)}) copy-start(s32[64]{0:T(128)} %param.10) | copy-start | bytes 772
  10.4 45.2 %copy-start.2 = (s32[128,2]{0,1:T(2,128)S(1)}, s32[128,2]{0,1:T(2,128)}, u32[]{:S(2)}) copy-start(s32[128,2]{0,1:T(2,128)} %param.9) | copy-start | bytes 3076
  192.5 61.9 %all-to-all-start.1 = ((bf16[64,5,2048]{2,1,0:T(8,128)(2,1)}), bf16[64,5,2048]{2,1,0:T(8,128)(2,1)}, u32[]{:S(2)}, u32[]{:S(2)}) async-start(bf16[64,5,2048]{2,1,0:T(8,128)(2,1)} %reshape.146), calls=%async_computation.1 | async-start | bytes 4194304 | tf_op jit(solution)/shard_map/all_to_all | solution.py:82
Sparse Core Ops, SparseCore 0:
  10.6 164.9 all-gather.5
where the time goes:
time: 273 us
  waiting for transfers between devices  107 us (39%)
  blocking collectives  96.3 us (35%)
  local copies, waits for them, and re-layouts  17.4 us (6%)
  matrix products  16.9 us (6%)
  between operations  15 us (5%)
  starting transfers between devices  10.8 us (4%)
  other arithmetic  9.2 us (3%)
    all_to_all x1, blocking collectives, local(): lax.all_to_all(outgoing, EXPERT, split_axis=0, concat_axis=0, tiled=True)  57.2 us
    all_gather x1, waiting for transfers between devices, gather_turned(): lax.all_gather(both, axis, axis=0, tiled=True)  56.2 us
    all_to_all x1, waiting for transfers between devices, local(): lax.all_to_all(answer, EXPERT, split_axis=0, concat_axis=0, tiled=True)  50.9 us
    all_gather x2, blocking collectives, carried_in(): pieces = lax.all_gather(total, axis)  29.1 us
    all_to_all x1, starting transfers between devices, local(): lax.all_to_all(answer, EXPERT, split_axis=0, concat_axis=0, tiled=True)  10.8 us
    unnamed x2, blocking collectives  9.97 us
    dot_general x1, matrix products, expert_rows(): lax.dot_general(hidden, down_w, (((1,), (1,)), ((), ())), preferred_eleme...  9.2 us
    dot_general x1, matrix products, expert_rows(): gate = jnp.dot(rows, gate_w, preferred_element_type=jnp.float32)  6.1 us
  transfers between devices with their start and end apart: 2, of which 2 were waited for; matrix products, arithmetic and copies ran while one was open for 4% of the time, Pallas kernels for 0%

commit v1 on v0

--- a/solution.py
+++ b/solution.py
@@ -6,6 +6,11 @@
 
 DP_EXPERT = ("dp", "expert_0", "expert_1", "expert_2")
 EXPERT = ("expert_0", "expert_1", "expert_2")
+
+
+def gather_over(x, name, along):
+    stack = jnp.stack([x] * lax.axis_size(name))
+    return jnp.concatenate(lax.all_to_all(stack, name, 0, 0), axis=along)
 
 
 def neutral_like(shard, identity):
@@ -30,7 +35,7 @@
 def gather_turned(arrays, axis, dims):
     turned = [jnp.moveaxis(a, dim, 0) for a, dim in zip(arrays, dims)]
     both = jnp.concatenate([t.reshape(len(t), -1) for t in turned], axis=1)
-    filled, at, finished = (lax.all_gather(both, axis, axis=0, tiled=True), 0, [])
+    filled, at, finished = (gather_over(both, axis, 0), 0, [])
     for t, dim in zip(turned, dims):
         piece = filled[:, at : at + t[0].size].reshape(-1, *t.shape[1:])
         finished.append(jnp.moveaxis(piece, 0, dim))

time: 273 us -> 397 us (1.45)
  waiting for transfers between devices: 107 us -> 285 us
  blocking collectives: 96.3 us -> 38.8 us
  between operations: 15 us -> 1.51 us
  starting transfers between devices: 10.8 us -> 20.1 us
  local copies, waits for them, and re-layouts: 17.4 us -> 24.6 us
    all_to_all x0 -> x2, waiting for transfers between devices: none -> 234 us  [the longest x1 187 us: gather_over(): return jnp.concatenate(lax.all_to_all(stack, name, 0, 0), axis=along)]
    all_to_all x1 -> x0, blocking collectives: 57.2 us -> none  [local(): lax.all_to_all(outgoing, EXPERT, split_axis=0, concat_axis=0, tiled=True)]
    all_gather x1 -> x0, waiting for transfers between devices: 56.2 us -> none  [gather_turned(): lax.all_gather(both, axis, axis=0, tiled=True)]
    all_to_all x0 -> x2, starting transfers between devices: none -> 13.1 us  [the longest x1 7.06 us: gather_over(): return jnp.concatenate(lax.all_to_all(stack, name, 0, 0), axis=along)]
    another operation x1 -> x2, local copies, waits for them, and re-layouts: 0.01 us -> 7.65 us  [the longest x1 7.65 us: gather_over(): stack = jnp.stack([x] * lax.axis_size(name))]
  transfers between devices with their start and end apart: 2 -> 3, of which waited for: 2 -> 3; matrix products, arithmetic and copies ran while one was open for 4% -> 1% of each run, Pallas kernels for 0% -> 0%
where the time goes in v1:
time: 397 us
  waiting for transfers between devices  285 us (72%)
  blocking collectives  38.8 us (10%)
  local copies, waits for them, and re-layouts  24.6 us (6%)
  starting transfers between devices  20.1 us (5%)
  matrix products  16.3 us (4%)
  other arithmetic  10.3 us (3%)
    all_to_all x1, waiting for transfers between devices, gather_over(): return jnp.concatenate(lax.all_to_all(stack, name, 0, 0), axis=along)  187 us
    all_to_all x1, waiting for transfers between devices, local(): lax.all_to_all(answer, EXPERT, split_axis=0, concat_axis=0, tiled=True)  50.9 us
    all_to_all x1, waiting for transfers between devices, local(): lax.all_to_all(outgoing, EXPERT, split_axis=0, concat_axis=0, tiled=True)  47.5 us
    all_gather x2, blocking collectives, carried_in(): pieces = lax.all_gather(total, axis)  28.8 us
    unnamed x2, blocking collectives  9.97 us
    dot_general x1, matrix products, expert_rows(): lax.dot_general(hidden, down_w, (((1,), (1,)), ((), ())), preferred_eleme...  9.2 us
  transfers between devices with their start and end apart: 3, of which 3 were waited for; matrix products, arithmetic and copies ran while one was open for 1% of the time, Pallas kernels for 0%

profile of v1, /device:TPU:8, one launch (start us, length us, event | category | flops | bytes accessed | tf_op | source)
XLA Modules:
  0.0 396.7 jit_solution(186294522271620228)
XLA Ops:
  0.0 0.8 copy.31
  1.2 1.3 dynamic-slice.1
  2.5 1.3 dynamic-slice
  5.2 0.2 dynamic-update-slice
  5.4 1.8 all-reduce
  7.3 0.2 fusion.26
  7.4 8.2 %all-reduce.1 = s32[256]{0:T(256)S(1)} all-reduce(s32[256]{0:T(256)S(1)} %fusion.26), channel_id=3, replica_groups=mesh['dp'=4,'expert_0'=8,'expert_1'=4,'expert_2'=2] {'expert_1'}, use_global_device_ids=true, to_apply=%add.1 | all-reduce | flops 256 | bytes 2048
  15.7 19.1 %all-gather.2 = s32[8,1,64]{2,1,0:T(1,128)S(1)} all-gather(s32[1,1,64]{2,1,0:T(1,128)S(1)} %fusion.32), channel_id=1, replica_groups=mesh['dp'=4,'expert_0'=8,'expert_1'=4,'expert_2'=2] {'expert_0'}, dimensions={0}, use_global_device_ids=true | all-gather | bytes 2304 | tf_op jit(solution)/shard_map/all_gather | solution.py:25
  34.8 9.7 %all-gather.3 = s32[4,1,64]{2,1,0:T(1,128)S(1)} all-gather(s32[1,1,64]{2,1,0:T(1,128)S(1)} %bitcast.111), channel_id=1, replica_groups=mesh['dp'=4,'expert_0'=8,'expert_1'=4,'expert_2'=2] {'dp'}, dimensions={0}, use_global_device_ids=true | all-gather | bytes 1280 | tf_op jit(solution)/shard_map/all_gather | solution.py:25
  44.5 0.6 reduce-window.6
  45.1 0.2 slice_reduce_fusion
  45.4 0.8 select_reduce_fusion.1
  46.5 0.2 reduce_sum.68
  47.0 0.7 multiply_select_fusion
  47.7 0.5 convolution_convert_fusion
  48.2 1.6 reshape.143
  49.8 6.0 %all-to-all-start = ((bf16[64,5,2048]{2,1,0:T(8,128)(2,1)}), bf16[64,5,2048]{2,1,0:T(8,128)(2,1)S(1)}, u32[]{:S(2)}, u32[]{:S(2)}) async-start(bf16[64,5,2048]{2,1,0:T(8,128)(2,1)} %reshape.143), calls=%async_computation | async-start | bytes 4194304 | tf_op jit(solution)/shard_map/all_to_all | solution.py:81
  55.9 3.8 pad_maximum_fusion
  59.6 47.5 %all-to-all-done = bf16[64,5,2048]{2,1,0:T(8,128)(2,1)S(1)} async-done(((bf16[64,5,2048]{2,1,0:T(8,128)(2,1)}), bf16[64,5,2048]{2,1,0:T(8,128)(2,1)S(1)}, u32[]{:S(2)}, u32[]{:S(2)}) %all-to-all-start) | async-done | bytes 1310752 | tf_op jit(solution)/shard_map/all_to_all | solution.py:81
  107.1 7.6 %stack.2 = bf16[4,352,6144]{2,1,0:T(8,128)(2,1)} broadcast(bf16[352,6144]{1,0:T(8,128)(2,1)} %pad_maximum_fusion), dimensions={1,2} | broadcast | bytes 21626880 | tf_op jit(solution)/shard_map/stack | solution.py:12
  114.8 7.1 %all-to-all-start.1 = ((bf16[4,352,6144]{2,1,0:T(8,128)(2,1)}), bf16[4,352,6144]{2,1,0:T(8,128)(2,1)}, u32[]{:S(2)}, u32[]{:S(2)}) async-start(bf16[4,352,6144]{2,1,0:T(8,128)(2,1)} %stack.2), calls=%async_computation.1 | async-start | bytes 34603008 | tf_op jit(solution)/shard_map/all_to_all | solution.py:13
  121.8 1.4 reshape.144
  123.2 186.7 %all-to-all-done.1 = bf16[4,352,6144]{2,1,0:T(8,128)(2,1)} async-done(((bf16[4,352,6144]{2,1,0:T(8,128)(2,1)}), bf16[4,352,6144]{2,1,0:T(8,128)(2,1)}, u32[]{:S(2)}, u32[]{:S(2)}) %all-to-all-start.1) | async-done | bytes 17301536 | tf_op jit(solution)/shard_map/all_to_all | solution.py:13
  309.9 6.6 %fusion.2 = f32[320,1408]{1,0:T(8,128)} fusion(bf16[320,2048]{1,0:T(8,128)(2,1)} %reshape.144, bf16[1408,6144]{1,0:T(8,128)(2,1)} %bitcast.21), kind=kOutput, calls=%fused_computation.6 | convolution fusion | flops 1845493760 | bytes 8880128 | tf_op jit(solution)/shard_map/dot_general | solution.py:47
  316.5 9.2 %fusion.4 = bf16[320,2048]{1,0:T(8,128)(2,1)S(1)} fusion(bf16[1408,6144]{1,0:T(8,128)(2,1)} %bitcast.21, bf16[320,2048]{1,0:T(8,128)(2,1)S(1)} %copy-done.1, f32[320,1408]{1,0:T(8,128)} %fusion.2), kind=kOutput, calls=%fused_computation.9 | convolution fusion | flops 3694346240 | bytes 15958016 | tf_op jit(solution)/shard_map/dot_general | solution.py:50
  325.7 1.6 reshape.152
  327.3 7.0 %all-to-all-start.2 = ((bf16[64,5,2048]{2,1,0:T(8,128)(2,1)}), bf16[64,5,2048]{2,1,0:T(8,128)(2,1)}, u32[]{:S(2)}, u32[]{:S(2)}) async-start(bf16[64,5,2048]{2,1,0:T(8,128)(2,1)} %reshape.152), calls=%async_computation.2 | async-start | bytes 4194304 | tf_op jit(solution)/shard_map/all_to_all | solution.py:87
  334.6 50.9 %all-to-all-done.2 = bf16[64,5,2048]{2,1,0:T(8,128)(2,1)} async-done(((bf16[64,5,2048]{2,1,0:T(8,128)(2,1)}), bf16[64,5,2048]{2,1,0:T(8,128)(2,1)}, u32[]{:S(2)}, u32[]{:S(2)}) %all-to-all-start.2) | async-done | bytes 1310752 | tf_op jit(solution)/shard_map/all_to_all | solution.py:87
  385.5 2.6 reshape.153
  388.0 2.3 gather_fusion
  390.4 2.4 reshape.154
  392.7 3.9 multiply_reduce_fusion
  (27 shorter events, 1.5 us)
Async XLA Ops:
  0.0 47.7 %copy-start = (bf16[128,2048]{1,0:T(8,128)(2,1)S(1)}, bf16[128,2048]{1,0:T(8,128)(2,1)}, u32[]{:S(2)}) copy-start(bf16[128,2048]{1,0:T(8,128)(2,1)} %param.7) | copy-start | bytes 1572868
  49.8 57.3 %all-to-all-start = ((bf16[64,5,2048]{2,1,0:T(8,128)(2,1)}), bf16[64,5,2048]{2,1,0:T(8,128)(2,1)S(1)}, u32[]{:S(2)}, u32[]{:S(2)}) async-start(bf16[64,5,2048]{2,1,0:T(8,128)(2,1)} %reshape.143), calls=%async_computation | async-start | bytes 4194304 | tf_op jit(solution)/shard_map/all_to_all | solution.py:81
  114.8 195.1 %all-to-all-start.1 = ((bf16[4,352,6144]{2,1,0:T(8,128)(2,1)}), bf16[4,352,6144]{2,1,0:T(8,128)(2,1)}, u32[]{:S(2)}, u32[]{:S(2)}) async-start(bf16[4,352,6144]{2,1,0:T(8,128)(2,1)} %stack.2), calls=%async_computation.1 | async-start | bytes 34603008 | tf_op jit(solution)/shard_map/all_to_all | solution.py:13
  309.9 6.6 %copy-start.1 = (bf16[320,2048]{1,0:T(8,128)(2,1)S(1)}, bf16[320,2048]{1,0:T(8,128)(2,1)}, u32[]{:S(2)}) copy-start(bf16[320,2048]{1,0:T(8,128)(2,1)} %reshape.144) | copy-start | bytes 3932164
  327.3 58.2 %all-to-all-start.2 = ((bf16[64,5,2048]{2,1,0:T(8,128)(2,1)}), bf16[64,5,2048]{2,1,0:T(8,128)(2,1)}, u32[]{:S(2)}, u32[]{:S(2)}) async-start(bf16[64,5,2048]{2,1,0:T(8,128)(2,1)} %reshape.152), calls=%async_computation.2 | async-start | bytes 4194304 | tf_op jit(solution)/shard_map/all_to_all | solution.py:87
